TPU v7x, 256 devices: a whole 4x4x8 slice. The times are simulated.
256 devices in a mesh: dp: 64 (over y, x_hi, z), mp: 4 (over x_lo, core).
Axes of the slice: x: 4 (x_hi: 2, x_lo: 2; x = x_hi * 2 + x_lo), y: 4, z: 8, core: 2. Of those that a mesh axis runs over, the one named last changes fastest.
Arguments:
- picture_skip_activations: bfloat16 [131072, 1152], P('dp'), as said below
- caption_closing_activations: bfloat16 [512, 1152], P('dp'), as said below
- normaliser_multipliers: float32 [3, 1152], replicated, may hold values from 0.1 to 1.9
- widening_matrix: bfloat16 [1152, 4304], P('dp', 'mp'), may hold values from -0.1875 to 0.1875
- contracting_matrix: bfloat16 [4304, 1152], P('mp', 'dp'), as said below
- caption_mapping_matrix: bfloat16 [1152, 1152], replicated, as said below
- sharpness_factor: float32 [1], replicated, may hold values from 8 to 32
- score_offset_term: float32 [1], replicated, may hold values from -8 to -3
Outputs:
- row_loss: float32 [512], P('dp')
- col_loss: float32 [512], P('dp')
Inputs may be any that keep to these rules, and one draw needn't show every extreme that they name: `picture_skip_activations`: entries lie within -8 and 8. `caption_closing_activations`: entries lie within -8 and 8. `contracting_matrix`: entries are at most 4.4 / sqrt(4304) in magnitude. `caption_mapping_matrix`: diagonal entries lie within 1 - 2.1 / sqrt(1152) and 1 + 2.1 / sqrt(1152), the others within -2.1 / sqrt(1152) and 2.1 / sqrt(1152).
All inputs are finite; a program needn't handle non-finite values.
Results may differ from a plain program's by a relative error of at most 0.01.
Values may be sent and summed in bfloat16 or wider, within the bound.
No kernel may reach another device: no remote copies, remote signals or barrier semaphores. Data moves between devices by JAX's collectives and lax.ppermute only.
A program may use at most 128 MiB of HBM per device.

v0:
```python
import jax
import jax.numpy as jnp
from jax import lax
from jax.sharding import Mesh
from jax.sharding import PartitionSpec as P

PATCHES = 256
DP = ("dp_0", "dp_1", "dp_2")


def joined_along(blocks, dim):
    blocks = jnp.moveaxis(blocks, 0, dim)
    shape = blocks.shape
    return blocks.reshape(*shape[:dim], shape[dim] * shape[dim + 1], *shape[dim + 2 :])


def stacked_from(array, axes, order):
    blocks = array
    for k in order:
        blocks = lax.all_gather(blocks, axes[k])
    done = order[::-1]
    back = [done.index(k) for k in range(len(axes))]
    blocks = blocks.transpose(*back, *range(len(axes), blocks.ndim))
    return blocks.reshape(-1, *array.shape)


def whole_of(array, axes, order, dim):
    return joined_along(stacked_from(array, axes, order), dim)


def split_up(array, dim, count):
    shape = array.shape
    blocks = array.reshape(*shape[:dim], count, shape[dim] // count, *shape[dim + 1 :])
    return jnp.moveaxis(blocks, dim, 0)


def sum_at_owner(array, axis, dim):
    blocks = split_up(array, dim, lax.axis_size(axis))
    arrived = lax.all_to_all(blocks, axis, split_axis=0, concat_axis=0, tiled=True)
    return arrived.astype(jnp.float32).sum(axis=0)


def from_everyone(array, axis):
    count = lax.axis_size(axis)
    return lax.all_to_all(
        jnp.broadcast_to(array[None], (count, *array.shape)), axis, 0, 0, tiled=True
    )


def gather_directly(array, axis, dim):
    blocks = from_everyone(array, axis)
    return joined_along(blocks, dim)


def sum_at_owner_2(array, axis, dim):
    count = lax.axis_size(axis)
    blocks = lax.all_to_all(split_up(array, dim, count), axis, 0, 0, tiled=True)
    return jnp.sum(blocks, axis=0)


def layer_norm(values, norm_gain):
    average = jnp.mean(values, axis=-1, keepdims=True)
    centred = values - average
    spread = jnp.mean(centred * centred, axis=-1, keepdims=True)
    return centred * lax.rsqrt(spread + 1e-06) * norm_gain


def unit_vector(vector):
    length = jnp.sqrt(jnp.sum(vector * vector, axis=-1, keepdims=True))
    return (vector / jnp.maximum(length, 1.0)).astype(jnp.bfloat16)


def pool_images(image_final):
    return jnp.mean(image_final.reshape(-1, PATCHES, image_final.shape[1]), axis=1)


def on_device(
    picture_skip_activations,
    caption_closing_activations,
    normaliser_multipliers,
    widening_matrix,
    contracting_matrix,
    caption_mapping_matrix,
    sharpness_factor,
    score_offset_term,
):
    image_rows = picture_skip_activations.astype(jnp.float32)
    image_normed = layer_norm(image_rows, normaliser_multipliers[0]).astype(jnp.bfloat16)
    inner_weight = whole_of(widening_matrix, DP, (1, 0, 2), 0)
    image_units = jax.nn.gelu(
        jnp.dot(image_normed, inner_weight, preferred_element_type=jnp.float32), approximate=True
    ).astype(jnp.bfloat16)
    partial_out = jnp.dot(
        image_units,
        lax.all_gather(contracting_matrix, DP, axis=1, tiled=True),
        preferred_element_type=jnp.float32,
    )
    unit_share = sum_at_owner(partial_out.astype(jnp.bfloat16), "mp", 0)
    own_count = unit_share.shape[0]
    own_first = lax.axis_index("mp") * own_count
    own_rows = lax.dynamic_slice_in_dim(image_rows, own_first, own_count, 0)
    image_final = layer_norm(own_rows + unit_share, normaliser_multipliers[1])
    own_emb = unit_vector(pool_images(image_final))
    picture_code_direction = gather_directly(own_emb, "mp", 0)
    text_normed = layer_norm(
        caption_closing_activations.astype(jnp.float32), normaliser_multipliers[2]
    ).astype(jnp.bfloat16)
    text_vector = jnp.dot(text_normed, caption_mapping_matrix, preferred_element_type=jnp.float32)
    caption_code_direction = unit_vector(text_vector)
    offset = lax.axis_index(DP) * picture_code_direction.shape[0]
    matching_scores = (
        sharpness_factor[0]
        * jnp.einsum(
            "pe,qe->pq",
            picture_code_direction,
            lax.all_gather(caption_code_direction, DP, axis=0, tiled=True),
            preferred_element_type=jnp.float32,
        )
        + score_offset_term[0]
    )
    row_index = offset + lax.broadcasted_iota(jnp.int32, matching_scores.shape, 0)
    col_index = lax.broadcasted_iota(jnp.int32, matching_scores.shape, 1)
    labels = jnp.where(row_index == col_index, 1.0, -1.0).astype(jnp.float32)
    loss_terms = jax.nn.softplus(-labels * matching_scores)
    row_loss = jnp.sum(loss_terms, axis=1)
    col_loss = sum_at_owner_2(jnp.sum(loss_terms, axis=0), DP, 0)
    return (row_loss, col_loss)


def solution(mesh):
    finer = Mesh(mesh.devices.reshape(4, 2, 8, mesh.shape["mp"]), ("dp_0", "dp_1", "dp_2", "mp"))
    in_specs = (P(DP, None), P(DP, None), P(), P(DP, "mp"), P("mp", DP), P(), P(), P())
    out_specs = (P(DP), P(DP))
    return jax.shard_map(
        on_device, mesh=finer, in_specs=in_specs, out_specs=out_specs, check_vma=False
    )
```

profile of v0, /device:TPU:2, one launch (start us, length us, event | category | flops | bytes accessed | tf_op | source)
XLA Modules:
  0.0 376.9 jit_solution(1932512164425936702)
XLA Ops:
  7.2 6.7 %all-gather.3 = bf16[2,18,1076]{2,1,0:T(8,128)(2,1)S(1)} all-gather(bf16[1,18,1076]{2,1,0:T(8,128)(2,1)} %bitcast.26), channel_id=2, replica_groups=mesh['dp_0'=4,'dp_1'=2,'dp_2'=8,'mp'=4] {'dp_1'}, dimensions={0}, use_global_device_ids=true | all-gather | bytes 116208 | tf_op jit(solution)/shard_map/all_gather | solution.py:20
  13.9 13.6 %all-gather.1 = bf16[8,18,1076]{2,1,0:T(8,128)(2,1)S(1)} all-gather(bf16[2,18,1076]{2,1,0:T(8,128)(2,1)S(1)} %all-gather.3), channel_id=3, replica_groups=mesh['dp_0'=4,'dp_1'=2,'dp_2'=8,'mp'=4] {'dp_0'}, dimensions={0}, use_global_device_ids=true | all-gather | bytes 387360 | tf_op jit(solution)/shard_map/all_gather | solution.py:20
  27.5 1.0 copy.15
  28.5 0.7 all-gather.13.cloned.1.call-update
  29.2 0.9 slice_reduce_fusion
  30.2 3.2 convert_reduce_fusion.1
  33.5 1.4 multiply_reduce_fusion
  34.9 37.8 %all-gather.11.cloned.1.call-done = bf16[32,2,18,1076]{3,1,2,0:T(2,128)(2,1)} async-done(((bf16[4,2,18,1076]{3,1,2,0:T(2,128)(2,1)}), bf16[32,2,18,1076]{3,1,2,0:T(2,128)(2,1)}) %all-gather.11.cloned.1.call-update) | async-done | bytes 2479120 | tf_op jit(solution)/shard_map/all_gather | solution.py:20
  72.7 4.0 %copy.16 = bf16[4,2,8,18,1076]{4,3,2,1,0:T(8,128)(2,1)} copy(bf16[4,2,8,18,1076]{4,1,3,0,2:T(2,128)(2,1)} %bitcast.22) | data formatting | bytes 4958208 | tf_op jit(solution)/shard_map/transpose | solution.py:23
  76.7 5.7 %reshape_reshape.3 = bf16[1152,1076]{1,0:T(8,128)(2,1)} reshape(bf16[4,2,8,18,1076]{4,3,2,1,0:T(8,128)(2,1)} %copy.16) | data formatting | bytes 4958208 | tf_op jit(solution)/shard_map/reshape;reshape | solution.py:14
  82.4 116.4 %all-gather.13.cloned.1.call-done = bf16[64,18,1076]{2,1,0:T(8,128)(2,1)} async-done(((bf16[1,18,1076]{2,1,0:T(8,128)(2,1)}), bf16[64,18,1076]{2,1,0:T(8,128)(2,1)}) %all-gather.13.cloned.1.call-update) | async-done | bytes 2479120 | tf_op jit(solution)/shard_map/all_gather | solution.py:95
  198.7 5.7 %reshape.91 = bf16[1152,1076]{1,0:T(8,128)(2,1)} reshape(bf16[64,18,1076]{2,1,0:T(8,128)(2,1)} %all-gather.13.cloned.1.call-done) | data formatting | bytes 4958208
  204.4 20.1 %convolution_convert_fusion = bf16[2048,1152]{1,0:T(8,128)(2,1)} fusion(bf16[1152,1076]{1,0:T(8,128)(2,1)} %reshape.91, bf16[1152,1076]{1,0:T(8,128)(2,1)} %reshape_reshape.3, bf16[2048,1152]{1,0:T(8,128)(2,1)} %param.8, f32[1152]{0:T(1024)S(1)} %get-tuple-element.3, f32[2048]{0:T(1024)S(1)} %add_rsqrt_fusion, f32[2048]{0:T(1024)S(1)} %broadcast_multiply_fusion), kind=kOutput, calls=%fused_computation.12 | convolution fusion | flops 10188398592 | bytes 14416384 | tf_op jit(solution)/shard_map/dot_general | solution.py:93
  224.5 6.7 %all-to-all-start = ((bf16[4,512,1152]{2,1,0:T(8,128)(2,1)}), bf16[4,512,1152]{2,1,0:T(8,128)(2,1)}, u32[]{:S(2)}, u32[]{:S(2)}) async-start(bf16[4,512,1152]{2,1,0:T(8,128)(2,1)} %bitcast.21), calls=%async_computation | async-start | bytes 9437184 | tf_op jit(solution)/shard_map/all_to_all | solution.py:39
  231.5 0.6 multiply_reduce_fusion.2
  232.1 0.7 divide_convert_fusion
  232.8 6.6 %convert_element_type.31 = f32[2048,1152]{1,0:T(8,128)} convert(bf16[2048,1152]{1,0:T(8,128)(2,1)} %param.8) | non-fusion elementwise | flops 2359296 | bytes 14155776 | tf_op jit(solution)/shard_map/convert_element_type | solution.py:87
  239.4 44.1 %all-to-all-done = bf16[4,512,1152]{2,1,0:T(8,128)(2,1)} async-done(((bf16[4,512,1152]{2,1,0:T(8,128)(2,1)}), bf16[4,512,1152]{2,1,0:T(8,128)(2,1)}, u32[]{:S(2)}, u32[]{:S(2)}) %all-to-all-start) | async-done | bytes 4718624 | tf_op jit(solution)/shard_map/all_to_all | solution.py:39
  283.5 3.3 convert_reduce_fusion
  286.9 2.2 fusion.29
  290.7 4.8 %all-to-all-start.1 = ((bf16[4,2,1152]{2,1,0:T(2,128)(2,1)}), bf16[4,2,1152]{2,1,0:T(2,128)(2,1)S(1)}, u32[]{:S(2)}, u32[]{:S(2)}) async-start(bf16[4,2,1152]{2,1,0:T(2,128)(2,1)} %broadcast_in_dim.10), calls=%async_computation.1 | async-start | bytes 36864 | tf_op jit(solution)/shard_map/all_to_all | solution.py:45
  297.4 50.1 %all-gather.9.cloned.1.call-done = bf16[512,1152]{1,0:T(8,128)(2,1)} async-done(((bf16[8,1152]{1,0:T(8,128)(2,1)}), bf16[512,1152]{1,0:T(8,128)(2,1)}) %all-gather.9.cloned.1.call-update) | async-done | bytes 1179664 | tf_op jit(solution)/shard_map/all_gather | solution.py:116
  347.6 2.3 fusion.28
  350.0 19.8 %all_to_all.19 = f32[64,1,8]{2,1,0:T(1,128)S(1)} all-to-all(f32[64,1,8]{2,1,0:T(1,128)S(1)} %bitcast.24), channel_id=1, replica_groups=mesh['dp_0'=4,'dp_1'=2,'dp_2'=8,'mp'=4] {'dp_0','dp_1','dp_2'}, dimensions={0} | all-to-all | bytes 4096 | tf_op jit(solution)/shard_map/all_to_all | solution.py:57
  (31 shorter events, 3.4 us)
Async XLA Ops:
  7.2 224.3 %copy-start = (bf16[1152,1152]{1,0:T(8,128)(2,1)S(1)}, bf16[1152,1152]{1,0:T(8,128)(2,1)}, u32[]{:S(2)}) copy-start(bf16[1152,1152]{1,0:T(8,128)(2,1)} %param.13) | copy-start | bytes 7962628
  7.2 65.5 %all-gather.11.cloned.1.call-start = ((), (), s32[]{:S(2)}) async-start(), calls=%async_computation.4 | async-start | bytes 2985984 | tf_op jit(solution)/shard_map/all_gather | solution.py:20
  28.5 170.3 %all-gather.13.cloned.1.call-start = ((), (), s32[]{:S(2)}) async-start(), calls=%async_computation.5 | async-start | bytes 3594240 | tf_op jit(solution)/shard_map/all_gather | solution.py:95
  29.2 4.2 %copy-start.1 = (bf16[2048,1152]{1,0:T(8,128)(2,1)S(1)}, bf16[2048,1152]{1,0:T(8,128)(2,1)}, u32[]{:S(2)}) copy-start(bf16[2048,1152]{1,0:T(8,128)(2,1)} %param.8) | copy-start | bytes 14155780
  224.5 6.7 %copy-start.2 = (bf16[8,1152]{1,0:T(8,128)(2,1)S(1)}, bf16[8,1152]{1,0:T(8,128)(2,1)}, u32[]{:S(2)}) copy-start(bf16[8,1152]{1,0:T(8,128)(2,1)} %param.9) | copy-start | bytes 55300
  224.5 59.1 %all-to-all-start = ((bf16[4,512,1152]{2,1,0:T(8,128)(2,1)}), bf16[4,512,1152]{2,1,0:T(8,128)(2,1)}, u32[]{:S(2)}, u32[]{:S(2)}) async-start(bf16[4,512,1152]{2,1,0:T(8,128)(2,1)} %bitcast.21), calls=%async_computation | async-start | bytes 9437184 | tf_op jit(solution)/shard_map/all_to_all | solution.py:39
  231.2 116.4 %all-gather.9.cloned.1.call-start = ((), (), s32[]{:S(2)}) async-start(), calls=%async_computation.3 | async-start | bytes 1198080 | tf_op jit(solution)/shard_map/all_gather | solution.py:116
  290.7 6.7 %all-to-all-start.1 = ((bf16[4,2,1152]{2,1,0:T(2,128)(2,1)}), bf16[4,2,1152]{2,1,0:T(2,128)(2,1)S(1)}, u32[]{:S(2)}, u32[]{:S(2)}) async-start(bf16[4,2,1152]{2,1,0:T(2,128)(2,1)} %broadcast_in_dim.10), calls=%async_computation.1 | async-start | bytes 36864 | tf_op jit(solution)/shard_map/all_to_all | solution.py:45
Sparse Core Ops, SparseCore 0:
  28.6 44.0 all-gather.10
  76.3 122.4 all-gather.12
  235.6 111.9 all-gather.8
where the time goes:
time: 378 us; the launch traced here: 377 us
  waiting for transfers between devices  250 us (66%)
  blocking collectives  40 us (11%)
  matrix products  23 us (6%)
  other arithmetic  19.4 us (5%)
  local copies, waits for them, and re-layouts  18 us (5%)
  between operations  15.1 us (4%)
  starting transfers between devices  11.6 us (3%)
    all_gather x1, waiting for transfers between devices, on_device(): lax.all_gather(contracting_matrix, DP, axis=1, tiled=True)  116 us
    all_gather x1, waiting for transfers between devices, on_device(): lax.all_gather(caption_code_direction, DP, axis=0, tiled=True)  50.1 us
    all_to_all x1, waiting for transfers between devices, sum_at_owner(): lax.all_to_all(blocks, axis, split_axis=0, concat_axis=0, tiled=True)  44.1 us
    all_gather x1, waiting for transfers between devices, stacked_from(): blocks = lax.all_gather(blocks, axes[k])  37.8 us
    all_gather x2, blocking collectives, stacked_from(): blocks = lax.all_gather(blocks, axes[k])  20.2 us
    dot_general x1, matrix products, on_device(): jnp.dot(image_units, lax.all_gather(contracting_matrix, DP, axis=1, tiled...  20.1 us
    all_to_all x1, blocking collectives, sum_at_owner_2(): blocks = lax.all_to_all(split_up(array, dim, count), axis, 0, 0, tiled=True)  19.8 us
  transfers between devices with their start and end apart: 5, of which 5 were waited for; matrix products, arithmetic and copies ran while one was open for 8% of the time, Pallas kernels for 0%

commit v1 on v0

--- a/solution.py
+++ b/solution.py
@@ -92,7 +92,9 @@
     ).astype(jnp.bfloat16)
     partial_out = jnp.dot(
         image_units,
-        lax.all_gather(contracting_matrix, DP, axis=1, tiled=True),
+        jnp.concatenate(
+            lax.all_to_all(jnp.stack([contracting_matrix] * lax.axis_size(DP)), DP, 0, 0), axis=1
+        ),
         preferred_element_type=jnp.float32,
     )
     unit_share = sum_at_owner(partial_out.astype(jnp.bfloat16), "mp", 0)

time: 378 us -> 321 us (0.85)
  waiting for transfers between devices: 250 us -> 165 us
  starting transfers between devices: 11.6 us -> 25.4 us
  blocking collectives: 40 us -> 48.1 us
    all_gather x1 -> x0, waiting for transfers between devices: 116 us -> none  [on_device(): lax.all_gather(contracting_matrix, DP, axis=1, tiled=True)]
    all_gather x1, waiting for transfers between devices: 37.8 us -> 68.3 us  [stacked_from(): blocks = lax.all_gather(blocks, axes[k])]
    all_to_all x0 -> x1, starting transfers between devices: none -> 14 us  [on_device(): lax.all_to_all(jnp.stack([contracting_matrix] * lax.axis_size(DP)), DP, 0...]
    all_gather x2, blocking collectives: 20.2 us -> 28.2 us  [stacked_from(): blocks = lax.all_gather(blocks, axes[k])]
    reshape x0 -> x1, local copies, waits for them, and re-layouts: none -> 5.65 us  [on_device(): jnp.concatenate(lax.all_to_all(jnp.stack([contracting_matrix] * lax.axis_...]
    unnamed x7 -> x8, local copies, waits for them, and re-layouts: 5.67 us -> 0.02 us
  transfers between devices with their start and end apart: 5 -> 5, of which waited for: 5 -> 4; matrix products, arithmetic and copies ran while one was open for 8% -> 10% of each run, Pallas kernels for 0% -> 0%
where the time goes in v1:
time: 321 us; the launch traced here: 320 us
  waiting for transfers between devices  165 us (51%)
  blocking collectives  48.1 us (15%)
  starting transfers between devices  25.4 us (8%)
  matrix products  23 us (7%)
  other arithmetic  21.5 us (7%)
  local copies, waits for them, and re-layouts  20.2 us (6%)
  between operations  16.9 us (5%)
    all_gather x1, waiting for transfers between devices, stacked_from(): blocks = lax.all_gather(blocks, axes[k])  68.3 us
    all_gather x1, waiting for transfers between devices, on_device(): lax.all_gather(caption_code_direction, DP, axis=0, tiled=True)  52.1 us
    all_to_all x1, waiting for transfers between devices, sum_at_owner(): lax.all_to_all(blocks, axis, split_axis=0, concat_axis=0, tiled=True)  44.1 us
    all_gather x2, blocking collectives, stacked_from(): blocks = lax.all_gather(blocks, axes[k])  28.2 us
    dot_general x1, matrix products, on_device(): jnp.dot(image_units, jnp.concatenate(lax.all_to_all(jnp.stack([contractin...  20.1 us
    all_to_all x1, blocking collectives, sum_at_owner_2(): blocks = lax.all_to_all(split_up(array, dim, count), axis, 0, 0, tiled=True)  19.9 us
    all_to_all x1, starting transfers between devices, on_device(): lax.all_to_all(jnp.stack([contracting_matrix] * lax.axis_size(DP)), DP, 0...  14 us
    convert_element_type x1, other arithmetic, on_device(): image_rows = picture_skip_activations.astype(jnp.float32)  6.57 us
  transfers between devices with their start and end apart: 5, of which 4 were waited for; matrix products, arithmetic and copies ran while one was open for 10% of the time, Pallas kernels for 0%

profile of v1, /device:TPU:2, one launch (start us, length us, event | category | flops | bytes accessed | tf_op | source)
XLA Modules:
  0.0 320.2 jit_solution(4552044341934933264)
XLA Ops:
  8.0 3.0 stack.2
  11.1 14.0 %all-to-all-start = ((bf16[64,1076,18]{1,2,0:T(8,128)(2,1)}), bf16[64,1076,18]{1,2,0:T(8,128)(2,1)}, u32[]{:S(2)}, u32[]{:S(2)}) async-start(bf16[64,1076,18]{1,2,0:T(8,128)(2,1)} %stack.2), calls=%async_computation | async-start | bytes 7077888 | tf_op jit(solution)/shard_map/all_to_all | solution.py:96
  25.2 12.9 %all-gather.3 = bf16[2,18,1076]{2,1,0:T(8,128)(2,1)S(1)} all-gather(bf16[1,18,1076]{2,1,0:T(8,128)(2,1)S(1)} %bitcast.25), channel_id=2, replica_groups=mesh['dp_0'=4,'dp_1'=2,'dp_2'=8,'mp'=4] {'dp_1'}, dimensions={0}, use_global_device_ids=true | all-gather | bytes 116208 | tf_op jit(solution)/shard_map/all_gather | solution.py:20
  38.1 15.3 %all-gather.1 = bf16[8,18,1076]{2,1,0:T(8,128)(2,1)S(1)} all-gather(bf16[2,18,1076]{2,1,0:T(8,128)(2,1)S(1)} %all-gather.3), channel_id=3, replica_groups=mesh['dp_0'=4,'dp_1'=2,'dp_2'=8,'mp'=4] {'dp_0'}, dimensions={0}, use_global_device_ids=true | all-gather | bytes 387360 | tf_op jit(solution)/shard_map/all_gather | solution.py:20
  53.4 1.0 copy.16
  54.4 3.0 convert_reduce_fusion.1
  57.5 3.7 %multiply_reduce_fusion = f32[2048]{0:T(1024)S(1)} fusion(bf16[2048,1152]{1,0:T(8,128)(2,1)} %param.8, f32[2048]{0:T(1024)S(1)} %broadcast_multiply_fusion), kind=kLoop, calls=%fused_computation.3 | loop fusion | flops 9435136 | bytes 4734976 | tf_op jit(solution)/shard_map/reduce_sum | solution.py:64
  61.2 68.3 %all-gather.9.cloned.1.call-done = bf16[32,2,18,1076]{3,1,2,0:T(2,128)(2,1)} async-done(((bf16[4,2,18,1076]{3,1,2,0:T(2,128)(2,1)}), bf16[32,2,18,1076]{3,1,2,0:T(2,128)(2,1)}) %all-gather.9.cloned.1.call-update) | async-done | bytes 2479120 | tf_op jit(solution)/shard_map/all_gather | solution.py:20
  129.5 4.0 %copy.17 = bf16[4,2,8,18,1076]{4,3,2,1,0:T(8,128)(2,1)} copy(bf16[4,2,8,18,1076]{4,1,3,0,2:T(2,128)(2,1)} %bitcast.22) | data formatting | bytes 4958208 | tf_op jit(solution)/shard_map/transpose | solution.py:23
  133.6 5.7 %reshape_reshape.3 = bf16[1152,1076]{1,0:T(8,128)(2,1)} reshape(bf16[4,2,8,18,1076]{4,3,2,1,0:T(8,128)(2,1)} %copy.17) | data formatting | bytes 4958208 | tf_op jit(solution)/shard_map/reshape;reshape | solution.py:14
  139.3 5.7 %reshape.91 = bf16[1076,1152]{0,1:T(8,128)(2,1)} reshape(bf16[1076,64,18]{0,2,1:T(8,128)(2,1)} %bitcast.5) | data formatting | bytes 4958208 | tf_op jit(solution)/shard_map/reshape | solution.py:95
  144.9 20.1 %convolution_convert_fusion = bf16[2048,1152]{1,0:T(8,128)(2,1)} fusion(bf16[1076,1152]{0,1:T(8,128)(2,1)} %reshape.91, bf16[1152,1076]{1,0:T(8,128)(2,1)} %reshape_reshape.3, bf16[2048,1152]{1,0:T(8,128)(2,1)} %param.8, f32[1152]{0:T(1024)S(1)} %get-tuple-element.3, f32[2048]{0:T(1024)S(1)} %add_rsqrt_fusion, f32[2048]{0:T(1024)S(1)} %broadcast_multiply_fusion), kind=kOutput, calls=%fused_computation.12 | convolution fusion | flops 10188398592 | bytes 14416384 | tf_op jit(solution)/shard_map/dot_general | solution.py:93
  165.0 6.5 %all-to-all-start.1 = ((bf16[4,512,1152]{2,1,0:T(8,128)(2,1)}), bf16[4,512,1152]{2,1,0:T(8,128)(2,1)}, u32[]{:S(2)}, u32[]{:S(2)}) async-start(bf16[4,512,1152]{2,1,0:T(8,128)(2,1)} %bitcast.21), calls=%async_computation.1 | async-start | bytes 9437184 | tf_op jit(solution)/shard_map/all_to_all | solution.py:39
  171.8 0.6 multiply_reduce_fusion.2
  172.5 0.7 divide_convert_fusion
  173.2 6.6 %convert_element_type.31 = f32[2048,1152]{1,0:T(8,128)} convert(bf16[2048,1152]{1,0:T(8,128)(2,1)} %param.8) | non-fusion elementwise | flops 2359296 | bytes 14155776 | tf_op jit(solution)/shard_map/convert_element_type | solution.py:87
  179.7 44.1 %all-to-all-done.1 = bf16[4,512,1152]{2,1,0:T(8,128)(2,1)} async-done(((bf16[4,512,1152]{2,1,0:T(8,128)(2,1)}), bf16[4,512,1152]{2,1,0:T(8,128)(2,1)}, u32[]{:S(2)}, u32[]{:S(2)}) %all-to-all-start.1) | async-done | bytes 4718624 | tf_op jit(solution)/shard_map/all_to_all | solution.py:39
  223.8 3.4 %convert_reduce_fusion = f32[512,1152]{1,0:T(8,128)S(1)} fusion(bf16[4,512,1152]{2,1,0:T(8,128)(2,1)} %all-to-all-done.1), kind=kLoop, calls=%fused_computation.1 | loop fusion | flops 4128768 | bytes 7077888 | tf_op jit(solution)/shard_map/reduce_sum | solution.py:40
  227.2 2.2 fusion.29
  230.4 0.6 broadcast_in_dim.10
  231.0 4.8 %all-to-all-start.2 = ((bf16[4,2,1152]{2,1,0:T(2,128)(2,1)}), bf16[4,2,1152]{2,1,0:T(2,128)(2,1)S(1)}, u32[]{:S(2)}, u32[]{:S(2)}) async-start(bf16[4,2,1152]{2,1,0:T(2,128)(2,1)} %broadcast_in_dim.10), calls=%async_computation.2 | async-start | bytes 36864 | tf_op jit(solution)/shard_map/all_to_all | solution.py:45
  237.7 52.1 %all-gather.7.cloned.1.call-done = bf16[512,1152]{1,0:T(8,128)(2,1)} async-done(((bf16[8,1152]{1,0:T(8,128)(2,1)}), bf16[512,1152]{1,0:T(8,128)(2,1)}) %all-gather.7.cloned.1.call-update) | async-done | bytes 1179664 | tf_op jit(solution)/shard_map/all_gather | solution.py:118
  289.9 2.3 fusion.28
  292.3 19.9 %all_to_all.24 = f32[64,1,8]{2,1,0:T(1,128)S(1)} all-to-all(f32[64,1,8]{2,1,0:T(1,128)S(1)} %bitcast.24), channel_id=1, replica_groups=mesh['dp_0'=4,'dp_1'=2,'dp_2'=8,'mp'=4] {'dp_0','dp_1','dp_2'}, dimensions={0} | all-to-all | bytes 4096 | tf_op jit(solution)/shard_map/all_to_all | solution.py:57
  (33 shorter events, 2.8 us)
Async XLA Ops:
  8.0 163.8 %copy-start = (bf16[1152,1152]{1,0:T(8,128)(2,1)S(1)}, bf16[1152,1152]{1,0:T(8,128)(2,1)}, u32[]{:S(2)}) copy-start(bf16[1152,1152]{1,0:T(8,128)(2,1)} %param.13) | copy-start | bytes 7962628
  8.0 17.1 %copy-start.2 = (bf16[18,1076]{1,0:T(8,128)(2,1)S(1)}, bf16[18,1076]{1,0:T(8,128)(2,1)}, u32[]{:S(2)}) copy-start(bf16[18,1076]{1,0:T(8,128)(2,1)} %param.11) | copy-start | bytes 116212
  11.1 43.3 %copy-start.3 = (f32[3,1152]{1,0:T(4,128)S(1)}, f32[3,1152]{1,0:T(4,128)}, u32[]{:S(2)}) copy-start(f32[3,1152]{1,0:T(4,128)} %param.10) | copy-start | bytes 41476
  11.1 128.2 %all-to-all-start = ((bf16[64,1076,18]{1,2,0:T(8,128)(2,1)}), bf16[64,1076,18]{1,2,0:T(8,128)(2,1)}, u32[]{:S(2)}, u32[]{:S(2)}) async-start(bf16[64,1076,18]{1,2,0:T(8,128)(2,1)} %stack.2), calls=%async_computation | async-start | bytes 7077888 | tf_op jit(solution)/shard_map/all_to_all | solution.py:96
  25.1 104.4 %all-gather.9.cloned.1.call-start = ((), (), s32[]{:S(2)}) async-start(), calls=%async_computation.5 | async-start | bytes 2985984 | tf_op jit(solution)/shard_map/all_gather | solution.py:20
  165.0 6.5 %copy-start.1 = (bf16[8,1152]{1,0:T(8,128)(2,1)S(1)}, bf16[8,1152]{1,0:T(8,128)(2,1)}, u32[]{:S(2)}) copy-start(bf16[8,1152]{1,0:T(8,128)(2,1)} %param.9) | copy-start | bytes 55300
  165.0 58.8 %all-to-all-start.1 = ((bf16[4,512,1152]{2,1,0:T(8,128)(2,1)}), bf16[4,512,1152]{2,1,0:T(8,128)(2,1)}, u32[]{:S(2)}, u32[]{:S(2)}) async-start(bf16[4,512,1152]{2,1,0:T(8,128)(2,1)} %bitcast.21), calls=%async_computation.1 | async-start | bytes 9437184 | tf_op jit(solution)/shard_map/all_to_all | solution.py:39
  171.5 118.4 %all-gather.7.cloned.1.call-start = ((), (), s32[]{:S(2)}) async-start(), calls=%async_computation.4 | async-start | bytes 1198080 | tf_op jit(solution)/shard_map/all_gather | solution.py:118
  231.0 6.7 %all-to-all-start.2 = ((bf16[4,2,1152]{2,1,0:T(2,128)(2,1)}), bf16[4,2,1152]{2,1,0:T(2,128)(2,1)S(1)}, u32[]{:S(2)}, u32[]{:S(2)}) async-start(bf16[4,2,1152]{2,1,0:T(2,128)(2,1)} %broadcast_in_dim.10), calls=%async_computation.2 | async-start | bytes 36864 | tf_op jit(solution)/shard_map/all_to_all | solution.py:45
Sparse Core Ops, SparseCore 0:
  54.5 74.9 all-gather.8
Sparse Core Ops, SparseCore 1:
  175.6 114.3 all-gather.6
